TPU v7x, 32 devices: a whole 2x2x4 slice. The times are simulated.
32 devices in a mesh: dp: 4 (over y, core), expert: 8 (over z, x).
Axes of the slice: x: 2, y: 2, z: 4, core: 2. Of those that a mesh axis runs over, the one named last changes fastest.
Arguments:
- tokens: bfloat16 [4096, 1024], P(('dp', 'expert')), may hold values from -6 to 6
- chosen_expert_index: int32 [4096, 6], P(('dp', 'expert')), may hold values from 0 to 7, as said below
- router_gate_weight: float32 [4096, 6], P(('dp', 'expert')), may hold values from 0.05 to 0.5
- output_gradient: bfloat16 [4096, 1024], P(('dp', 'expert')), may hold values from -0.15917969 to 0.15917969
- gate_weight_matrix: bfloat16 [8, 1024, 704], P('expert'), may hold values from -0.1875 to 0.1875
- up_weight: bfloat16 [8, 1024, 704], P('expert'), may hold values from -0.1875 to 0.1875
- down_weight: bfloat16 [8, 704, 1024], P('expert'), may hold values from -0.21875 to 0.21875
- adapter_down_maps: bfloat16 [8, 16, 704], P('expert'), may hold values from -0.21875 to 0.21875
- adapter_up_maps: bfloat16 [8, 16, 1024], P('expert'), may hold values from -1.5 to 1.5
Outputs:
- mixed: bfloat16 [4096, 1024], P(('dp', 'expert'))
- grad_in: bfloat16 [8, 16, 704], P('expert')
- grad_out: bfloat16 [8, 16, 1024], P('expert')
Inputs may be any that keep to these rules, and one draw needn't show every extreme that they name: `chosen_expert_index`: each row names 6 different experts. In each aligned block of 128 rows (the rows of one device) no expert is named by more than 126 rows, and one and the same expert, drawn for the whole array, is named by exactly 126 rows of every block. Each row's experts are 6 neighbours in one circular order of all experts, drawn for the whole array.
All inputs are finite; a program needn't handle non-finite values.
Results may differ from a plain program's by a relative error of at most 0.0064.
Values may be sent and summed in bfloat16 or wider, within the bound.
A program may use at most 64 MiB of HBM per device.

v0:
```python
import jax
import jax.numpy as jnp
from jax import lax
from jax.sharding import PartitionSpec as P


def shards(
    tokens,
    chosen_expert_index,
    router_gate_weight,
    output_gradient,
    gate_weight_matrix,
    up_weight,
    down_weight,
    adapter_down_maps,
    adapter_up_maps,
):
    tok_rows, model_width = tokens.shape
    top_count = chosen_expert_index.shape[1]
    adapter_depth = adapter_down_maps.shape[1]
    hidden_width = gate_weight_matrix.shape[2]
    held_experts = gate_weight_matrix.shape[0]
    experts = lax.axis_size("expert") * held_experts
    most_hot = min(2 * tok_rows // experts, tok_rows // top_count)
    slot_cap = top_count * most_hot
    total_slots = tok_rows * top_count
    flat_ids = chosen_expert_index.reshape(total_slots)
    onehot = (flat_ids[:, None] == jnp.arange(experts, dtype=jnp.int32)[None, :]).astype(jnp.int32)
    slot_rank = jnp.sum((jnp.cumsum(onehot, axis=0) - onehot) * onehot, axis=1)
    slot_place = flat_ids * slot_cap + slot_rank
    source_slot = (
        jnp.full((experts * slot_cap,), -1, jnp.int32)
        .at[slot_place]
        .set(jnp.arange(total_slots, dtype=jnp.int32))
    )
    filled = source_slot >= 0
    safe_slot = jnp.maximum(source_slot, 0)
    source_token = safe_slot // top_count
    send_rows = jnp.where(filled[:, None], tokens[source_token], jnp.zeros((), tokens.dtype))
    send_rows = send_rows.reshape(experts, slot_cap, model_width)
    buffer_gates = jnp.where(
        filled, router_gate_weight.reshape(total_slots)[safe_slot], jnp.float32(0.0)
    )
    grad_rows = (buffer_gates[:, None] * output_gradient[source_token].astype(jnp.float32)).astype(
        jnp.bfloat16
    )
    grad_rows = grad_rows.reshape(experts, slot_cap, model_width)
    slot_rows = lax.all_to_all(send_rows, "expert", split_axis=0, concat_axis=0, tiled=True)
    source_count = slot_rows.shape[0]
    item_count = slot_rows.shape[1]
    flat_rows = slot_rows.reshape(source_count * item_count, model_width)
    gate_proj = jnp.dot(flat_rows, gate_weight_matrix[0], preferred_element_type=jnp.float32)
    upward = jnp.dot(flat_rows, up_weight[0], preferred_element_type=jnp.float32)
    hidden_state = (jax.nn.silu(gate_proj) * upward).astype(jnp.bfloat16)
    rank_state = jnp.dot(
        hidden_state, adapter_down_maps[0].T, preferred_element_type=jnp.float32
    ).astype(jnp.bfloat16)
    output = (
        jnp.dot(hidden_state, down_weight[0], preferred_element_type=jnp.float32)
        + jnp.dot(rank_state, adapter_up_maps[0], preferred_element_type=jnp.float32)
    ).astype(jnp.bfloat16)
    output, rank_state, hidden_state = (
        output.reshape(source_count, item_count, model_width),
        rank_state.reshape(source_count, item_count, adapter_depth),
        hidden_state.reshape(source_count, item_count, hidden_width),
    )
    returned = lax.all_to_all(output, "expert", split_axis=0, concat_axis=0, tiled=True)
    slot_out = returned.reshape(experts * slot_cap, model_width)[slot_place].astype(jnp.float32)
    mixed = jnp.sum(
        slot_out.reshape(tok_rows, top_count, model_width) * router_gate_weight[:, :, None], axis=1
    )
    mixed = mixed.astype(jnp.bfloat16)
    recv_grads = lax.all_to_all(grad_rows, "expert", split_axis=0, concat_axis=0, tiled=True)
    flattened_gradient = recv_grads.reshape(-1, model_width)
    received_rank_gradient = jnp.dot(
        flattened_gradient, adapter_up_maps[0].T, preferred_element_type=jnp.float32
    ).astype(jnp.bfloat16)
    grad_model = jnp.dot(
        rank_state.reshape(-1, adapter_depth).T,
        flattened_gradient,
        preferred_element_type=jnp.float32,
    )
    grad_hidden = jnp.dot(
        received_rank_gradient.T,
        hidden_state.reshape(-1, hidden_width),
        preferred_element_type=jnp.float32,
    )
    summed_hidden, summed_model = lax.psum((grad_hidden, grad_model), "dp")
    return (
        mixed,
        summed_hidden.astype(jnp.bfloat16)[None],
        summed_model.astype(jnp.bfloat16)[None],
    )


def solution(mesh):
    return jax.shard_map(
        shards,
        mesh=mesh,
        in_specs=(
            P(("dp", "expert"), None),
            P(("dp", "expert"), None),
            P(("dp", "expert"), None),
            P(("dp", "expert"), None),
            P("expert", None, None),
            P("expert", None, None),
            P("expert", None, None),
            P("expert", None, None),
            P("expert", None, None),
        ),
        out_specs=(P(("dp", "expert"), None), P("expert", None, None), P("expert", None, None)),
        check_vma=False,
    )
```

profile of v0, /device:TPU:1, one launch (start us, length us, event | category | flops | bytes accessed | tf_op | source)
XLA Modules:
  0.0 196.2 jit_solution(2679010438886048528)
XLA Ops:
  0.6 0.9 copy.16
  2.5 1.7 reduce-window.6
  5.1 3.4 %scatter_custom_fusion = s32[1008]{0:T(1024)S(1)} fusion(s32[768]{0:T(1024)S(1)} %fusion.14, s32[768]{0:T(1024)S(1)} %iota.11, s32[]{:T(128)} %constant.10.clone.1), kind=kCustom, calls=%fused_computation.43 | custom fusion | bytes 4036 | tf_op jit(solution)/shard_map/scatter | solution.py:34
  8.5 0.8 copy.20
  9.9 4.5 %gather_fusion.2 = f32[1008]{0:T(1024)S(1)} fusion(f32[768]{0:T(1024)S(1)} %reshape.94, s32[1024]{0:T(1024)S(1)} %get-tuple-element.9), kind=kCustom, calls=%fused_computation.2 | custom fusion | bytes 12096 | tf_op jit(solution)/shard_map/gather | solution.py:42
  14.5 5.3 %gather_fusion = bf16[1008,1024]{1,0:T(8,128)(2,1)} fusion(bf16[128,1024]{1,0:T(8,128)(2,1)S(1)} %copy-done.1, s32[1024]{0:T(1024)S(1)} %get-tuple-element.10), kind=kCustom, calls=%fused_computation | custom fusion | bytes 4132800 | tf_op jit(solution)/shard_map/gather | solution.py:39
  19.9 1.8 gather.15
  21.7 1.6 broadcast_select_fusion
  23.3 6.5 %all-to-all-start = ((bf16[8,126,1024]{2,1,0:T(8,128)(2,1)}), bf16[8,126,1024]{2,1,0:T(8,128)(2,1)}, u32[]{:S(2)}, u32[]{:S(2)}) async-start(bf16[8,126,1024]{2,1,0:T(8,128)(2,1)} %broadcast_select_fusion), calls=%async_computation | async-start | bytes 4194304 | tf_op jit(solution)/shard_map/all_to_all | solution.py:48
  29.8 5.4 %gather_fusion.3 = bf16[1008,1024]{1,0:T(8,128)(2,1)} fusion(bf16[128,1024]{1,0:T(8,128)(2,1)S(1)} %copy-done.2, s32[1024]{0:T(1024)S(1)} %get-tuple-element.10), kind=kCustom, calls=%fused_computation.3 | custom fusion | bytes 4132800 | tf_op jit(solution)/shard_map/gather | solution.py:44
  35.2 3.4 %reshape.97 = f32[8,126,1024]{2,1,0:T(8,128)} reshape(bf16[1008,1024]{1,0:T(8,128)(2,1)} %gather_fusion.3) | data formatting | bytes 6193152 | tf_op jit(solution)/shard_map/convert_element_type | solution.py:44
  38.6 3.8 %multiply_convert_fusion = bf16[8,126,1024]{2,1,0:T(8,128)(2,1)} fusion(f32[8,126,1024]{2,1,0:T(8,128)} %reshape.97, f32[8,126]{1,0:T(8,128)S(1)} %mul.53), kind=kLoop, calls=%fused_computation.5 | loop fusion | flops 2064384 | bytes 6197184 | tf_op jit(solution)/shard_map/convert_element_type | solution.py:44
  42.4 34.9 %all-to-all-done = bf16[8,126,1024]{2,1,0:T(8,128)(2,1)} async-done(((bf16[8,126,1024]{2,1,0:T(8,128)(2,1)}), bf16[8,126,1024]{2,1,0:T(8,128)(2,1)}, u32[]{:S(2)}, u32[]{:S(2)}) %all-to-all-start) | async-done | bytes 2064416 | tf_op jit(solution)/shard_map/all_to_all | solution.py:48
  77.3 4.6 %all-to-all-start.2 = ((bf16[8,126,1024]{2,1,0:T(8,128)(2,1)}), bf16[8,126,1024]{2,1,0:T(8,128)(2,1)S(1)}, u32[]{:S(2)}, u32[]{:S(2)}) async-start(bf16[8,126,1024]{2,1,0:T(8,128)(2,1)} %multiply_convert_fusion), calls=%async_computation.2 | async-start | bytes 4194304 | tf_op jit(solution)/shard_map/all_to_all | solution.py:73
  81.9 2.8 %reshape.91 = bf16[1008,1024]{1,0:T(8,128)(2,1)} reshape(bf16[8,126,1024]{2,1,0:T(8,128)(2,1)} %all-to-all-done) | data formatting | bytes 4128768 | tf_op jit(solution)/shard_map/reshape | solution.py:51
  84.8 3.8 %fusion.3 = f32[1008,704]{0,1:T(8,128)S(1)} fusion(bf16[1008,1024]{1,0:T(8,128)(2,1)} %reshape.91, bf16[1,1024,704]{1,2,0:T(8,128)(2,1)} %param.13), kind=kOutput, calls=%fused_computation.13 | convolution fusion | flops 1453326336 | bytes 6344704 | tf_op jit(solution)/shard_map/dot_general | solution.py:52
  88.6 1.9 multiply_convert_fusion.1
  90.9 1.8 fusion
  92.7 2.0 %add_convert_fusion = bf16[1008,1024]{1,0:T(8,128)(2,1)} fusion(f32[1008,1024]{1,0:T(8,128)S(1)} %fusion, bf16[1008,16]{0,1:T(8,128)(2,1)S(1)} %convolution_convert_fusion.1, bf16[1,16,1024]{2,1,0:T(8,128)(2,1)S(1)} %copy-done.10), kind=kOutput, calls=%fused_computation.7 | convolution fusion | flops 35094528 | bytes 6258176 | tf_op jit(solution)/shard_map/dot_general | solution.py:60
  94.8 2.8 %reshape.92 = bf16[8,126,1024]{2,1,0:T(8,128)(2,1)} reshape(bf16[1008,1024]{1,0:T(8,128)(2,1)} %add_convert_fusion) | data formatting | bytes 4128768 | tf_op jit(solution)/shard_map/reshape | solution.py:63
  97.6 31.9 %all-to-all-done.2 = bf16[8,126,1024]{2,1,0:T(8,128)(2,1)S(1)} async-done(((bf16[8,126,1024]{2,1,0:T(8,128)(2,1)}), bf16[8,126,1024]{2,1,0:T(8,128)(2,1)S(1)}, u32[]{:S(2)}, u32[]{:S(2)}) %all-to-all-start.2) | async-done | bytes 2064416 | tf_op jit(solution)/shard_map/all_to_all | solution.py:73
  129.5 1.3 copy-done.3
  130.8 4.5 %all-to-all-start.1 = ((bf16[8,126,1024]{2,1,0:T(8,128)(2,1)}), bf16[8,126,1024]{2,1,0:T(8,128)(2,1)}, u32[]{:S(2)}, u32[]{:S(2)}) async-start(bf16[8,126,1024]{2,1,0:T(8,128)(2,1)} %reshape.92), calls=%async_computation.1 | async-start | bytes 4194304 | tf_op jit(solution)/shard_map/all_to_all | solution.py:67
  136.0 1.8 reshape.95
  137.8 1.0 fusion.17
  138.9 3.0 %fusion.5 = f32[16,704]{1,0:T(8,128)S(1)} fusion(bf16[1008,704]{0,1:T(8,128)(2,1)} %copy-done.4, bf16[1008,1024]{1,0:T(8,128)(2,1)S(1)} %reshape.95, bf16[1,16,1024]{2,1,0:T(8,128)(2,1)} %param.17), kind=kOutput, calls=%fused_computation.16 | convolution fusion | flops 55754496 | bytes 3561472 | tf_op jit(solution)/shard_map/dot_general | solution.py:83
  141.8 14.3 %all-reduce = (bf16[16,704]{1,0:T(8,128)(2,1)}, bf16[16,1024]{1,0:T(8,128)(2,1)}) all-reduce(f32[16,704]{1,0:T(8,128)S(1)} %fusion.5, f32[16,1024]{1,0:T(8,128)} %fusion.17), channel_id=1, replica_groups=mesh['dp'=4,'expert'=8] {'dp'}, use_global_device_ids=true, to_apply=%region_5.6 | all-reduce | flops 27648 | bytes 165888 | tf_op jit(solution)/shard_map/psum | solution.py:88
  156.1 26.4 %all-to-all-done.1 = bf16[8,126,1024]{2,1,0:T(8,128)(2,1)} async-done(((bf16[8,126,1024]{2,1,0:T(8,128)(2,1)}), bf16[8,126,1024]{2,1,0:T(8,128)(2,1)}, u32[]{:S(2)}, u32[]{:S(2)}) %all-to-all-start.1) | async-done | bytes 2064416 | tf_op jit(solution)/shard_map/all_to_all | solution.py:67
  182.5 1.8 reshape.93
  184.3 3.6 %gather_fusion.1 = bf16[768,1024]{1,0:T(8,128)(2,1)} fusion(bf16[1008,1024]{1,0:T(8,128)(2,1)S(1)} %reshape.93, s32[1024]{0:T(1024)S(1)} %copy-done.12), kind=kCustom, calls=%fused_computation.1 | custom fusion | bytes 3148800 | tf_op jit(solution)/shard_map/gather | solution.py:68
  187.9 3.9 %reshape.96 = f32[128,6,1024]{2,1,0:T(8,128)} reshape(bf16[768,1024]{1,0:T(8,128)(2,1)} %gather_fusion.1) | data formatting | bytes 4718592 | tf_op jit(solution)/shard_map/convert_element_type | solution.py:68
  191.9 4.3 %multiply_reduce_fusion = bf16[128,1024]{1,0:T(8,128)(2,1)} fusion(f32[128,6,1024]{2,1,0:T(8,128)} %reshape.96, f32[128,6]{1,0:T(8,128)S(1)} %copy-done.7), kind=kLoop, calls=%fused_computation.6 | loop fusion | flops 1441792 | bytes 3410944 | tf_op jit(solution)/shard_map/reduce_sum | solution.py:69
  (48 shorter events, 3.5 us)
Async XLA Ops:
  0.6 90.2 %copy-start = (bf16[1,704,1024]{2,1,0:T(8,128)(2,1)S(1)}, bf16[1,704,1024]{2,1,0:T(8,128)(2,1)}, u32[]{:S(2)}) copy-start(bf16[1,704,1024]{2,1,0:T(8,128)(2,1)} %param.15) | copy-start | bytes 4325380
  9.3 0.6 copy-start.6
  9.9 4.6 %copy-start.1 = (bf16[128,1024]{1,0:T(8,128)(2,1)S(1)}, bf16[128,1024]{1,0:T(8,128)(2,1)}, u32[]{:S(2)}) copy-start(bf16[128,1024]{1,0:T(8,128)(2,1)} %param.9) | copy-start | bytes 786436
  23.3 6.6 %copy-start.2 = (bf16[128,1024]{1,0:T(8,128)(2,1)S(1)}, bf16[128,1024]{1,0:T(8,128)(2,1)}, u32[]{:S(2)}) copy-start(bf16[128,1024]{1,0:T(8,128)(2,1)} %param.12) | copy-start | bytes 786436
  23.3 54.0 %all-to-all-start = ((bf16[8,126,1024]{2,1,0:T(8,128)(2,1)}), bf16[8,126,1024]{2,1,0:T(8,128)(2,1)}, u32[]{:S(2)}, u32[]{:S(2)}) async-start(bf16[8,126,1024]{2,1,0:T(8,128)(2,1)} %broadcast_select_fusion), calls=%async_computation | async-start | bytes 4194304 | tf_op jit(solution)/shard_map/all_to_all | solution.py:48
  77.3 52.2 %all-to-all-start.2 = ((bf16[8,126,1024]{2,1,0:T(8,128)(2,1)}), bf16[8,126,1024]{2,1,0:T(8,128)(2,1)S(1)}, u32[]{:S(2)}, u32[]{:S(2)}) async-start(bf16[8,126,1024]{2,1,0:T(8,128)(2,1)} %multiply_convert_fusion), calls=%async_computation.2 | async-start | bytes 4194304 | tf_op jit(solution)/shard_map/all_to_all | solution.py:73
  84.8 3.8 %copy-start.5 = (bf16[1008,1024]{1,0:T(8,128)(2,1)S(1)}, bf16[1008,1024]{1,0:T(8,128)(2,1)}, u32[]{:S(2)}) copy-start(bf16[1008,1024]{1,0:T(8,128)(2,1)} %reshape.91) | copy-start | bytes 6193156
  84.8 3.8 %copy-start.13 = (bf16[1,1024,704]{1,2,0:T(8,128)(2,1)S(1)}, bf16[1,1024,704]{1,2,0:T(8,128)(2,1)}, u32[]{:S(2)}) copy-start(bf16[1,1024,704]{1,2,0:T(8,128)(2,1)} %param.14) | copy-start | bytes 4325380
  88.6 1.9 copy-start.11
  90.5 2.2 %copy-start.4 = (bf16[1008,704]{0,1:T(8,128)(2,1)}, bf16[1008,704]{0,1:T(8,128)(2,1)S(1)}, u32[]{:S(2)}) copy-start(bf16[1008,704]{0,1:T(8,128)(2,1)S(1)} %multiply_convert_fusion.1) | copy-start | bytes 4257796
  90.9 1.9 copy-start.8
  90.9 1.9 copy-start.10
  129.5 1.3 copy-start.3
  130.8 51.6 %all-to-all-start.1 = ((bf16[8,126,1024]{2,1,0:T(8,128)(2,1)}), bf16[8,126,1024]{2,1,0:T(8,128)(2,1)}, u32[]{:S(2)}, u32[]{:S(2)}) async-start(bf16[8,126,1024]{2,1,0:T(8,128)(2,1)} %reshape.92), calls=%async_computation.1 | async-start | bytes 4194304 | tf_op jit(solution)/shard_map/all_to_all | solution.py:67
  136.0 1.8 copy-start.9
  156.1 28.2 %copy-start.12 = (s32[1024]{0:T(1024)S(1)}, s32[1024]{0:T(1024)}, u32[]{:S(2)}) copy-start(s32[1024]{0:T(1024)} %pad_clamp_fusion.1) | copy-start | bytes 12292
  187.9 3.9 %copy-start.7 = (f32[128,6]{1,0:T(8,128)S(1)}, f32[128,6]{1,0:T(8,128)}, u32[]{:S(2)}) copy-start(f32[128,6]{1,0:T(8,128)} %copy-done.6) | copy-start | bytes 9220
where the time goes:
time: 199 us; the launch traced here: 196 us
  waiting for transfers between devices  93.2 us (47%)
  local copies, waits for them, and re-layouts  45.3 us (23%)
  starting transfers between devices  15.6 us (8%)
  blocking collectives  14.3 us (7%)
  matrix products  13.9 us (7%)
  other arithmetic  13 us (7%)
    all_to_all x1, waiting for transfers between devices, shards(): lax.all_to_all(send_rows, 'expert', split_axis=0, concat_axis=0, tiled=True)  34.9 us
    all_to_all x1, waiting for transfers between devices, shards(): lax.all_to_all(grad_rows, 'expert', split_axis=0, concat_axis=0, tiled=True)  31.9 us
    all_to_all x1, waiting for transfers between devices, shards(): lax.all_to_all(output, 'expert', split_axis=0, concat_axis=0, tiled=True)  26.4 us
    psum x1, blocking collectives, shards(): summed_hidden, summed_model = lax.psum((grad_hidden, grad_model), 'dp')  14.3 us
    gather x2, local copies, waits for them, and re-layouts, shards(): tokens[source_token]  7.15 us
    all_to_all x1, starting transfers between devices, shards(): lax.all_to_all(send_rows, 'expert', split_axis=0, concat_axis=0, tiled=True)  6.47 us
    gather x1, local copies, waits for them, and re-layouts, shards(): output_gradient[source_token].astype(jnp.float32)  5.35 us
    all_to_all x1, starting transfers between devices, shards(): lax.all_to_all(grad_rows, 'expert', split_axis=0, concat_axis=0, tiled=True)  4.63 us
  transfers between devices with their start and end apart: 3, of which 3 were waited for; matrix products, arithmetic and copies ran while one was open for 18% of the time, Pallas kernels for 0%

commit v1 on v0

v1 whole, which is shorter than its diff:
```python
import functools

import jax
import jax.numpy as jnp
from jax import lax
from jax.experimental import pallas as pl
from jax.experimental.pallas import tpu as pltpu
from jax.sharding import PartitionSpec as P

MESH = pl.DeviceIdType.MESH
F32 = jnp.float32
BF16 = jnp.bfloat16


def dot_nt(a, b):
    return lax.dot_general(a, b, (((1,), (1,)), ((), ())), preferred_element_type=F32)


def dot(a, b):
    return jnp.dot(a, b, preferred_element_type=F32)


def kernel(
    n,
    nd,
    tok_h,
    idx_ref,
    w_ref,
    og_ref,
    gw_h,
    uw_h,
    dw_h,
    ad_ref,
    au_ref,
    mixed_ref,
    gin_ref,
    gout_ref,
    tok_all,
    gw,
    uw,
    dw,
    hid_all,
    out_send,
    out_recv,
    au_all,
    lg_send,
    lg_recv,
    rk_send,
    rk_recv,
    gexp,
    gp_send,
    gp_recv,
    gin_all,
    gout_all,
    acc,
    loc_sem,
    tok_s,
    tok_r,
    au_s,
    au_r,
    lg_s,
    lg_r,
    rk_s,
    rk_r,
    out_s,
    out_r,
    gp_s,
    gp_r,
    gin_s,
    gin_r,
    gout_s,
    gout_r,
):
    me = lax.axis_index("expert")
    rep = lax.axis_index("dp")
    rows = tok_all.shape[1]
    rank = ad_ref.shape[1]
    width = tok_all.shape[2]

    def peer(s):
        return lax.rem(me + s, n)

    def source(s):
        return lax.rem(me + n - s, n)

    def mate(s):
        return lax.rem(rep + s, nd)

    def to_expert(src, dst, s_sem, r_sem, p):
        return pltpu.make_async_remote_copy(
            src_ref=src,
            dst_ref=dst,
            send_sem=s_sem,
            recv_sem=r_sem,
            device_id={"expert": p},
            device_id_type=MESH,
        )

    def to_mate(src, dst, s_sem, r_sem, p):
        return pltpu.make_async_remote_copy(
            src_ref=src,
            dst_ref=dst,
            send_sem=s_sem,
            recv_sem=r_sem,
            device_id={"dp": p},
            device_id_type=MESH,
        )

    def each(lo, hi, fn):
        def body(s, carry):
            fn(s)
            return carry

        lax.fori_loop(lo, hi, body, 0)

    load_tok = pltpu.make_async_copy(tok_h, tok_all.at[me], loc_sem.at[0])
    load_gw = pltpu.make_async_copy(gw_h.at[0], gw, loc_sem.at[1])
    load_uw = pltpu.make_async_copy(uw_h.at[0], uw, loc_sem.at[2])
    load_dw = pltpu.make_async_copy(dw_h.at[0], dw, loc_sem.at[3])
    load_tok.start()
    load_gw.start()
    load_uw.start()
    load_dw.start()

    barrier = pltpu.get_barrier_semaphore()
    each(
        1,
        n,
        lambda s: pl.semaphore_signal(
            barrier, inc=1, device_id={"expert": peer(s)}, device_id_type=MESH
        ),
    )
    each(
        1,
        nd,
        lambda s: pl.semaphore_signal(
            barrier, inc=1, device_id={"dp": mate(s)}, device_id_type=MESH
        ),
    )
    pl.semaphore_wait(barrier, n - 1 + nd - 1)

    def au_copy(s):
        p = peer(s)
        return to_expert(au_ref.at[0], au_all.at[me], au_s.at[p], au_r.at[me], p)

    def tok_copy(s):
        p = peer(s)
        return to_expert(tok_all.at[me], tok_all.at[me], tok_s.at[p], tok_r.at[me], p)

    def lg_copy(s):
        p = peer(s)
        return to_expert(lg_send.at[p], lg_recv.at[me], lg_s.at[p], lg_r.at[me], p)

    def rk_copy(p):
        return to_expert(rk_send.at[p], rk_recv.at[me], rk_s.at[p], rk_r.at[me], p)

    def out_copy(p):
        return to_expert(out_send.at[p], out_recv.at[me], out_s.at[p], out_r.at[me], p)

    def gp_copy(p):
        return to_expert(gp_send.at[p], gp_recv.at[me], gp_s.at[p], gp_r.at[me], p)

    def gin_copy(s):
        p = mate(s)
        return to_mate(gin_all.at[rep], gin_all.at[rep], gin_s.at[p], gin_r.at[rep], p)

    def gout_copy(s):
        p = mate(s)
        return to_mate(gout_all.at[rep], gout_all.at[rep], gout_s.at[p], gout_r.at[rep], p)

    def arrived(buf, sems, p):
        to_expert(buf.at[p], buf.at[p], sems.at[p], sems.at[p], p).wait_recv()

    def arrived_mate(buf, sems, p):
        to_mate(buf.at[p], buf.at[p], sems.at[p], sems.at[p], p).wait_recv()

    each(1, n, lambda s: au_copy(s).start())
    load_tok.wait()
    each(1, n, lambda s: tok_copy(s).start())
    au_all[me] = au_ref[0]

    eye = lax.broadcasted_iota(jnp.int32, (rows, rows), 0) == lax.broadcasted_iota(
        jnp.int32, (rows, rows), 1
    )

    def gate_column(e):
        return jnp.sum(jnp.where(idx_ref[...] == e, w_ref[...], 0.0), axis=1, keepdims=True)

    def spread_gates(e):
        row = jnp.sum(jnp.where(eye, gate_column(e), 0.0), axis=0, keepdims=True)
        gexp[e] = jnp.broadcast_to(row, (rank, rows))

    each(0, n, spread_gates)

    load_gw.wait()
    load_uw.wait()
    load_dw.wait()

    def expert_block(src):
        x = tok_all[src]
        g = dot(x, gw[...])
        u = dot(x, uw[...])
        h = (g / (1.0 + jnp.exp(-g)) * u).astype(BF16)
        hid_all[src] = h
        low_t = dot_nt(ad_ref[0], h).astype(BF16)
        low = dot_nt(h, ad_ref[0]).astype(BF16)
        out = (dot(h, dw[...]) + dot(low, au_ref[0])).astype(BF16)
        return low_t, out

    low_t, out = expert_block(me)
    rk_recv[me] = low_t
    out_recv[me] = out

    each(1, n, lambda s: arrived(au_all, au_r, source(s)))
    low_grad = dot_nt(au_all[...].reshape(n * rank, width), og_ref[...])
    low_grad = low_grad * gexp[...].reshape(n * rank, rows)
    lg_send[...] = low_grad.astype(BF16).reshape(n, rank, rows)
    lg_recv[me] = lg_send[me]
    each(1, n, lambda s: lg_copy(s).start())

    def step(s):
        src = source(s)
        arrived(tok_all, tok_r, src)
        low_t, out = expert_block(src)
        rk_send[src] = low_t
        out_send[src] = out
        rk_copy(src).start()
        out_copy(src).start()

    each(1, n, step)

    each(1, n, lambda s: arrived(lg_recv, lg_r, source(s)))

    def add_gin(src, total):
        return total + dot(lg_recv[src], hid_all[src])

    gin_all[rep] = lax.fori_loop(0, n, add_gin, jnp.zeros(gin_all.shape[1:], F32))

    each(1, n, lambda s: arrived(rk_recv, rk_r, source(s)))
    low_w = (rk_recv[...].astype(F32) * gexp[...]).astype(BF16).reshape(n * rank, rows)
    gp = dot(low_w, og_ref[...])
    gp_send[...] = gp.astype(BF16).reshape(n, rank, width)
    each(1, nd, lambda s: gin_copy(s).start())
    gp_recv[me] = gp_send[me]
    each(1, n, lambda s: gp_copy(peer(s)).start())

    acc[...] = gate_column(me) * out_recv[me].astype(F32)

    def combine(s):
        e = source(s)
        arrived(out_recv, out_r, e)
        acc[...] += gate_column(e) * out_recv[e].astype(F32)

    each(1, n, combine)
    mixed_ref[...] = acc[...].astype(BF16)

    each(1, n, lambda s: arrived(gp_recv, gp_r, source(s)))
    gout_all[rep] = jnp.sum(gp_recv[...].astype(F32), axis=0)
    each(1, nd, lambda s: arrived_mate(gin_all, gin_r, mate(s)))
    gin_ref[0] = jnp.sum(gin_all[...], axis=0).astype(BF16)
    each(1, nd, lambda s: gout_copy(s).start())
    each(1, nd, lambda s: arrived_mate(gout_all, gout_r, mate(s)))
    gout_ref[0] = jnp.sum(gout_all[...], axis=0).astype(BF16)

    def drain(s):
        au_copy(s).wait_send()
        tok_copy(s).wait_send()
        lg_copy(s).wait_send()
        p = peer(s)
        rk_copy(p).wait_send()
        out_copy(p).wait_send()
        gp_copy(p).wait_send()

    each(1, n, drain)

    def drain_mates(s):
        gin_copy(s).wait_send()
        gout_copy(s).wait_send()

    each(1, nd, drain_mates)


def shards(
    n,
    nd,
    tokens,
    chosen_expert_index,
    router_gate_weight,
    output_gradient,
    gate_weight_matrix,
    up_weight,
    down_weight,
    adapter_down_maps,
    adapter_up_maps,
):
    rows, width = tokens.shape
    rank, hidden = adapter_down_maps.shape[1:]
    vmem = pl.BlockSpec(memory_space=pltpu.VMEM)
    anywhere = pl.BlockSpec(memory_space=pl.ANY)
    dma = pltpu.SemaphoreType.DMA
    return pl.pallas_call(
        functools.partial(kernel, n, nd),
        out_shape=(
            jax.ShapeDtypeStruct((rows, width), BF16),
            jax.ShapeDtypeStruct((1, rank, hidden), BF16),
            jax.ShapeDtypeStruct((1, rank, width), BF16),
        ),
        in_specs=[anywhere, vmem, vmem, vmem, anywhere, anywhere, anywhere, vmem, vmem],
        out_specs=(vmem, vmem, vmem),
        scratch_shapes=[
            pltpu.VMEM((n, rows, width), BF16),
            pltpu.VMEM((width, hidden), BF16),
            pltpu.VMEM((width, hidden), BF16),
            pltpu.VMEM((hidden, width), BF16),
            pltpu.VMEM((n, rows, hidden), BF16),
            pltpu.VMEM((n, rows, width), BF16),
            pltpu.VMEM((n, rows, width), BF16),
            pltpu.VMEM((n, rank, width), BF16),
            pltpu.VMEM((n, rank, rows), BF16),
            pltpu.VMEM((n, rank, rows), BF16),
            pltpu.VMEM((n, rank, rows), BF16),
            pltpu.VMEM((n, rank, rows), BF16),
            pltpu.VMEM((n, rank, rows), F32),
            pltpu.VMEM((n, rank, width), BF16),
            pltpu.VMEM((n, rank, width), BF16),
            pltpu.VMEM((nd, rank, hidden), F32),
            pltpu.VMEM((nd, rank, width), F32),
            pltpu.VMEM((rows, width), F32),
            dma((4,)),
        ]
        + [dma((n,))] * 12
        + [dma((nd,))] * 4,
        compiler_params=pltpu.CompilerParams(
            collective_id=0, has_side_effects=True, vmem_limit_bytes=60 * 1024 * 1024
        ),
    )(
        tokens,
        chosen_expert_index,
        router_gate_weight,
        output_gradient,
        gate_weight_matrix,
        up_weight,
        down_weight,
        adapter_down_maps,
        adapter_up_maps,
    )


def solution(mesh):
    return jax.shard_map(
        functools.partial(shards, mesh.shape["expert"], mesh.shape["dp"]),
        mesh=mesh,
        in_specs=(
            P(("dp", "expert"), None),
            P(("dp", "expert"), None),
            P(("dp", "expert"), None),
            P(("dp", "expert"), None),
            P("expert", None, None),
            P("expert", None, None),
            P("expert", None, None),
            P("expert", None, None),
            P("expert", None, None),
        ),
        out_specs=(P(("dp", "expert"), None), P("expert", None, None), P("expert", None, None)),
        check_vma=False,
    )
```

time: 199 us -> 135 us (0.68); the launches traced: 196 us -> 135 us
  Pallas kernels: 0 us -> 123 us
  waiting for transfers between devices: 93.2 us -> 0 us
  local copies, waits for them, and re-layouts: 45.3 us -> 11.5 us
  starting transfers between devices: 15.6 us -> 0 us
  blocking collectives: 14.3 us -> 0 us
  matrix products: 13.9 us -> 0 us
  other arithmetic: 13 us -> 0 us
    pallas_call x0 -> x1, Pallas kernels: none -> 123 us  [shards(): pl.pallas_call(functools.partial(kernel, n, nd), out_shape=(jax.ShapeDtyp...]
    all_to_all x3 -> x0, waiting for transfers between devices: 93.2 us -> none  [the longest x1 34.9 us: shards(): lax.all_to_all(send_rows, 'expert', split_axis=0, concat_axis=0, tiled=True)]
    gather x5 -> x0, local copies, waits for them, and re-layouts: 20.6 us -> none  [the longest x2 7.15 us: shards(): tokens[source_token]]
    all_to_all x3 -> x0, starting transfers between devices: 15.6 us -> none  [the longest x1 6.47 us: shards(): lax.all_to_all(send_rows, 'expert', split_axis=0, concat_axis=0, tiled=True)]
    psum x1 -> x0, blocking collectives: 14.3 us -> none  [shards(): summed_hidden, summed_model = lax.psum((grad_hidden, grad_model), 'dp')]
    dot_general x7 -> x0, matrix products: 13.9 us -> none  [the longest x1 3.82 us: shards(): jnp.dot(flat_rows, gate_weight_matrix[0], preferred_element_type=jnp.floa...]
    reshape x5 -> x0, local copies, waits for them, and re-layouts: 9.45 us -> none  [the longest x1 2.83 us: shards(): flat_rows = slot_rows.reshape(source_count * item_count, model_width)]
    unnamed x30 -> x9, local copies, waits for them, and re-layouts: 3.55 us -> 11.5 us
  transfers between devices with their start and end apart: 3 -> 0, of which waited for: 3 -> 0; matrix products, arithmetic and copies ran while one was open for 18% -> 0% of each run, Pallas kernels for 0% -> 0%
where the time goes in v1:
time: 135 us
  Pallas kernels  123 us (91%)
  local copies, waits for them, and re-layouts  11.5 us (9%)
    pallas_call x1, Pallas kernels, shards(): pl.pallas_call(functools.partial(kernel, n, nd), out_shape=(jax.ShapeDtyp...  123 us
    unnamed x9, local copies, waits for them, and re-layouts  11.5 us

profile of v1, /device:TPU:1, one launch (start us, length us, event | category | flops | bytes accessed | tf_op | source)
XLA Modules:
  0.0 135.0 jit_solution(5921066508922720964)
XLA Ops:
  0.6 1.4 %copy.12.idx_ref = s32[128,6]{1,0:T(8,128)} copy(s32[128,6]{0,1:T(8,128)} %param.10) | data formatting | bytes 6144 | tf_op args[1]
  2.1 1.4 %copy.13.w_ref = f32[128,6]{1,0:T(8,128)} copy(f32[128,6]{0,1:T(8,128)} %param.11) | data formatting | bytes 6144 | tf_op args[2]
  3.5 0.0 copy-start
  3.5 2.7 %copy.14.gw_h = bf16[1,1024,704]{2,1,0:T(8,128)(2,1)} copy(bf16[1,1024,704]{1,2,0:T(8,128)(2,1)} %param.13) | data formatting | bytes 2883584 | tf_op args[4]
  6.2 0.0 copy-done
  6.2 1.6 %copy.15.uw_h = bf16[1,1024,704]{2,1,0:T(8,128)(2,1)} copy(bf16[1,1024,704]{1,2,0:T(8,128)(2,1)S(1)} %copy-done) | data formatting | bytes 2883584 | tf_op args[5]
  7.7 122.8 %shard_map.112 = (bf16[128,1024]{1,0:T(8,128)(2,1)}, bf16[1,16,704]{2,1,0:T(8,128)(2,1)}, bf16[1,16,1024]{2,1,0:T(8,128)(2,1)}) custom-call(bf16[128,1024]{1,0:T(8,128)(2,1)} %tok_h.1, s32[128,6]{1,0:T(8,128)} %copy.12.idx_ref, f32[128,6]{1,0:T(8,128)} %copy.13.w_ref, bf16[128,1024]{1,0:T(8,128)(2,1)} %og_ref.1, bf16[1,1024,704]{2,1,0:T(8,128)(2,1)} %copy.14.gw_h, ...), custom_call_target="tpu_custom_call" | custom-call | tf_op jit(solution)/shard_map/pallas_call | solution.py:301
  130.6 1.7 %copy.19 = bf16[128,1024]{1,0:T(8,128)(2,1)} copy(bf16[128,1024]{1,0:T(8,128)(2,1)} %get-tuple-element.6) | data formatting | bytes 524288
  132.2 1.3 copy.20
  133.6 1.4 %copy.21 = bf16[1,16,1024]{2,1,0:T(8,128)(2,1)} copy(bf16[1,16,1024]{2,1,0:T(8,128)(2,1)} %get-tuple-element.8) | data formatting | bytes 65536
Async XLA Ops:
  3.5 2.7 %copy-start = (bf16[1,1024,704]{1,2,0:T(8,128)(2,1)S(1)}, bf16[1,1024,704]{1,2,0:T(8,128)(2,1)}, u32[]{:S(2)}) copy-start(bf16[1,1024,704]{1,2,0:T(8,128)(2,1)} %param.14) | copy-start | bytes 4325380

commit v2 on v1

--- a/solution.py
+++ b/solution.py
@@ -41,7 +41,10 @@
     dw,
     hid_all,
     out_send,
-    out_recv,
+    pair_recv,
+    line_send,
+    line_recv,
+    gate_recv,
     au_all,
     lg_send,
     lg_recv,
@@ -54,16 +57,22 @@
     gout_all,
     acc,
     loc_sem,
-    tok_s,
+    up_s,
+    down_s,
+    side_s,
     tok_r,
+    gate_s,
+    gate_r,
     au_s,
     au_r,
     lg_s,
     lg_r,
     rk_s,
     rk_r,
-    out_s,
-    out_r,
+    pair_s,
+    pair_r,
+    line_s,
+    line_r,
     gp_s,
     gp_r,
     gin_s,
@@ -73,6 +82,10 @@
 ):
     me = lax.axis_index("expert")
     rep = lax.axis_index("dp")
+    line = 4 if n % 4 == 0 else n
+    side = n // line
+    at_line = me // side
+    at_side = lax.rem(me, side)
     rows = tok_all.shape[1]
     rank = ad_ref.shape[1]
     width = tok_all.shape[2]
@@ -121,6 +134,17 @@
     load_gw.start()
     load_uw.start()
     load_dw.start()
+
+    eye = lax.broadcasted_iota(jnp.int32, (rows, rows), 0) == lax.broadcasted_iota(
+        jnp.int32, (rows, rows), 1
+    )
+
+    def spread_gates(e):
+        column = jnp.sum(jnp.where(idx_ref[...] == e, w_ref[...], 0.0), axis=1, keepdims=True)
+        row = jnp.sum(jnp.where(eye, column, 0.0), axis=0, keepdims=True)
+        gexp[e] = jnp.broadcast_to(row, (rank, rows))
+
+    each(0, n, spread_gates)
 
     barrier = pltpu.get_barrier_semaphore()
     each(
@@ -143,9 +167,41 @@
         p = peer(s)
         return to_expert(au_ref.at[0], au_all.at[me], au_s.at[p], au_r.at[me], p)
 
-    def tok_copy(s):
+    def up_copy(z):
+        k = z * side + at_side
+        p = (at_line + 1) * side + at_side
+        return to_expert(tok_all.at[k], tok_all.at[k], up_s.at[z], tok_r.at[k], p)
+
+    def down_copy(z):
+        k = z * side + at_side
+        p = (at_line - 1) * side + at_side
+        return to_expert(tok_all.at[k], tok_all.at[k], down_s.at[z], tok_r.at[k], p)
+
+    def side_copy(z, s):
+        k = z * side + at_side
+        x = lax.rem(at_side + s, side)
+        p = at_line * side + x
+        return to_expert(tok_all.at[k], tok_all.at[k], side_s.at[z * side + x], tok_r.at[k], p)
+
+    def gate_copy(s):
         p = peer(s)
-        return to_expert(tok_all.at[me], tok_all.at[me], tok_s.at[p], tok_r.at[me], p)
+        return to_expert(
+            gexp.at[p, pl.ds(0, 8)], gate_recv.at[me], gate_s.at[p], gate_r.at[me], p
+        )
+
+    def pair_copy(z, x):
+        k = z * side + x
+        p = at_line * side + x
+        return to_expert(
+            out_send.at[k], pair_recv.at[z * side + at_side], pair_s.at[k],
+            pair_r.at[z * side + at_side], p,
+        )
+
+    def line_copy(z):
+        p = z * side + at_side
+        return to_expert(
+            line_send.at[z], line_recv.at[at_line], line_s.at[z], line_r.at[at_line], p
+        )
 
     def lg_copy(s):
         p = peer(s)
@@ -154,9 +210,6 @@
     def rk_copy(p):
         return to_expert(rk_send.at[p], rk_recv.at[me], rk_s.at[p], rk_r.at[me], p)
 
-    def out_copy(p):
-        return to_expert(out_send.at[p], out_recv.at[me], out_s.at[p], out_r.at[me], p)
-
     def gp_copy(p):
         return to_expert(gp_send.at[p], gp_recv.at[me], gp_s.at[p], gp_r.at[me], p)
 
@@ -174,23 +227,24 @@
     def arrived_mate(buf, sems, p):
         to_mate(buf.at[p], buf.at[p], sems.at[p], sems.at[p], p).wait_recv()
 
+    each(1, n, lambda s: gate_copy(s).start())
     each(1, n, lambda s: au_copy(s).start())
     load_tok.wait()
-    each(1, n, lambda s: tok_copy(s).start())
+
+    def spread(z, go_up, go_down):
+        @pl.when(go_up & (at_line + 1 < line))
+        def _():
+            up_copy(z).start()
+
+        @pl.when(go_down & (at_line >= 1))
+        def _():
+            down_copy(z).start()
+
+        each(1, side, lambda s: side_copy(z, s).start())
+
+    spread(at_line, True, True)
     au_all[me] = au_ref[0]
-
-    eye = lax.broadcasted_iota(jnp.int32, (rows, rows), 0) == lax.broadcasted_iota(
-        jnp.int32, (rows, rows), 1
-    )
-
-    def gate_column(e):
-        return jnp.sum(jnp.where(idx_ref[...] == e, w_ref[...], 0.0), axis=1, keepdims=True)
-
-    def spread_gates(e):
-        row = jnp.sum(jnp.where(eye, gate_column(e), 0.0), axis=0, keepdims=True)
-        gexp[e] = jnp.broadcast_to(row, (rank, rows))
-
-    each(0, n, spread_gates)
+    gate_recv[me] = gexp[me, 0:8]
 
     load_gw.wait()
     load_uw.wait()
@@ -207,27 +261,97 @@
         out = (dot(h, dw[...]) + dot(low, au_ref[0])).astype(BF16)
         return low_t, out
 
-    low_t, out = expert_block(me)
-    rk_recv[me] = low_t
-    out_recv[me] = out
-
-    each(1, n, lambda s: arrived(au_all, au_r, source(s)))
-    low_grad = dot_nt(au_all[...].reshape(n * rank, width), og_ref[...])
-    low_grad = low_grad * gexp[...].reshape(n * rank, rows)
-    lg_send[...] = low_grad.astype(BF16).reshape(n, rank, rows)
-    lg_recv[me] = lg_send[me]
-    each(1, n, lambda s: lg_copy(s).start())
-
-    def step(s):
-        src = source(s)
-        arrived(tok_all, tok_r, src)
-        low_t, out = expert_block(src)
-        rk_send[src] = low_t
-        out_send[src] = out
-        rk_copy(src).start()
-        out_copy(src).start()
-
-    each(1, n, step)
+    def low_grads():
+        each(1, n, lambda s: arrived(au_all, au_r, source(s)))
+        low_grad = dot_nt(au_all[...].reshape(n * rank, width), og_ref[...])
+        low_grad = low_grad * gexp[...].reshape(n * rank, rows)
+        lg_send[...] = low_grad.astype(BF16).reshape(n, rank, rows)
+        lg_recv[me] = lg_send[me]
+        each(1, n, lambda s: lg_copy(s).start())
+
+    def on_line(z):
+        return (z >= 0) & (z < line)
+
+    def relay(k):
+        for sign in (-1, 1):
+            z = at_line + sign * k
+
+            @pl.when((k >= 1) & on_line(z))
+            def _():
+                arrived(tok_all, tok_r, z * side + at_side)
+                spread(z, sign < 0, sign > 0)
+
+    def work(k, j):
+        s = j // 2
+        sign = 1 - 2 * lax.rem(j, 2)
+        far = k - jnp.minimum(s, 1)
+        z = at_line + sign * far
+        x = lax.rem(at_side + s, side)
+        src = z * side + x
+
+        @pl.when(on_line(z) & (far >= 0) & ((far > 0) | (sign > 0)))
+        def _():
+            @pl.when(s > 0)
+            def _():
+                arrived(tok_all, tok_r, src)
+
+            @pl.when(src != me)
+            def _():
+                arrived(gate_recv, gate_r, src)
+
+            low_t, out = expert_block(src)
+            row = gate_recv[src, 0:1]
+            column = jnp.sum(jnp.where(eye, row, 0.0), axis=1, keepdims=True)
+            term = (out.astype(F32) * column).astype(BF16)
+
+            @pl.when(s > 0)
+            def _():
+                out_send[src] = term
+
+            @pl.when(s == 0)
+            def _():
+                pair_recv[src] = term
+
+            @pl.when(src == me)
+            def _():
+                rk_recv[me] = low_t
+
+            @pl.when(src != me)
+            def _():
+                rk_send[src] = low_t
+                rk_copy(src).start()
+
+            @pl.when(s > 0)
+            def _():
+                pair_copy(z, x).start()
+
+    def pair_sum(z):
+        def wait_pair(s):
+            arrived(pair_recv, pair_r, z * side + lax.rem(at_side + s, side))
+
+        each(1, side, wait_pair)
+
+        def add(x, total):
+            return total + pair_recv[z * side + x].astype(F32)
+
+        return lax.fori_loop(1, side, add, pair_recv[z * side].astype(F32))
+
+    def combine(k):
+        for sign in (-1, 1):
+            z = at_line + sign * (k - 2)
+
+            @pl.when((k >= 3) & on_line(z))
+            def _():
+                line_send[z] = pair_sum(z).astype(BF16)
+                line_copy(z).start()
+
+    def step(k):
+        relay(k)
+        each(0, 2 * side, lambda j: work(k, j))
+        pl.when(k == 0)(low_grads)
+        combine(k)
+
+    each(0, line + 2, step)
 
     each(1, n, lambda s: arrived(lg_recv, lg_r, source(s)))
 
@@ -244,14 +368,14 @@
     gp_recv[me] = gp_send[me]
     each(1, n, lambda s: gp_copy(peer(s)).start())
 
-    acc[...] = gate_column(me) * out_recv[me].astype(F32)
-
-    def combine(s):
-        e = source(s)
-        arrived(out_recv, out_r, e)
-        acc[...] += gate_column(e) * out_recv[e].astype(F32)
-
-    each(1, n, combine)
+    acc[...] = pair_sum(at_line)
+
+    def finish(t):
+        z = lax.rem(at_line + t, line)
+        arrived(line_recv, line_r, z)
+        acc[...] += line_recv[z].astype(F32)
+
+    each(1, line, finish)
     mixed_ref[...] = acc[...].astype(BF16)
 
     each(1, n, lambda s: arrived(gp_recv, gp_r, source(s)))
@@ -264,14 +388,34 @@
 
     def drain(s):
         au_copy(s).wait_send()
-        tok_copy(s).wait_send()
+        gate_copy(s).wait_send()
         lg_copy(s).wait_send()
         p = peer(s)
         rk_copy(p).wait_send()
-        out_copy(p).wait_send()
         gp_copy(p).wait_send()
 
     each(1, n, drain)
+
+    def drain_line(z):
+        @pl.when((z <= at_line) & (at_line + 1 < line))
+        def _():
+            up_copy(z).wait_send()
+
+        @pl.when((z >= at_line) & (at_line >= 1))
+        def _():
+            down_copy(z).wait_send()
+
+        def drain_side(s):
+            side_copy(z, s).wait_send()
+            pair_copy(z, lax.rem(at_side + s, side)).wait_send()
+
+        each(1, side, drain_side)
+
+        @pl.when(z != at_line)
+        def _():
+            line_copy(z).wait_send()
+
+    each(0, line, drain_line)
 
     def drain_mates(s):
         gin_copy(s).wait_send()
@@ -295,6 +439,7 @@
 ):
     rows, width = tokens.shape
     rank, hidden = adapter_down_maps.shape[1:]
+    line = 4 if n % 4 == 0 else n
     vmem = pl.BlockSpec(memory_space=pltpu.VMEM)
     anywhere = pl.BlockSpec(memory_space=pl.ANY)
     dma = pltpu.SemaphoreType.DMA
@@ -315,6 +460,9 @@
             pltpu.VMEM((n, rows, hidden), BF16),
             pltpu.VMEM((n, rows, width), BF16),
             pltpu.VMEM((n, rows, width), BF16),
+            pltpu.VMEM((line, rows, width), BF16),
+            pltpu.VMEM((line, rows, width), BF16),
+            pltpu.VMEM((n, 8, rows), F32),
             pltpu.VMEM((n, rank, width), BF16),
             pltpu.VMEM((n, rank, rows), BF16),
             pltpu.VMEM((n, rank, rows), BF16),
@@ -328,7 +476,10 @@
             pltpu.VMEM((rows, width), F32),
             dma((4,)),
         ]
+        + [dma((line,))] * 2
         + [dma((n,))] * 12
+        + [dma((line,))] * 2
+        + [dma((n,))] * 2
         + [dma((nd,))] * 4,
         compiler_params=pltpu.CompilerParams(
             collective_id=0, has_side_effects=True, vmem_limit_bytes=60 * 1024 * 1024

time: 135 us -> 101 us (0.75)
  Pallas kernels: 123 us -> 88.8 us
    pallas_call x1, Pallas kernels: 123 us -> 88.8 us  [shards(): pl.pallas_call(functools.partial(kernel, n, nd), out_shape=(jax.ShapeDtyp...]
where the time goes in v2:
time: 101 us
  Pallas kernels  88.8 us (88%)
  local copies, waits for them, and re-layouts  11.5 us (11%)
    pallas_call x1, Pallas kernels, shards(): pl.pallas_call(functools.partial(kernel, n, nd), out_shape=(jax.ShapeDtyp...  88.8 us
    unnamed x9, local copies, waits for them, and re-layouts  11.5 us

profile of v2, /device:TPU:1, one launch (start us, length us, event | category | flops | bytes accessed | tf_op | source)
XLA Modules:
  0.0 100.9 jit_solution(3384294196119863334)
XLA Ops:
  0.6 1.4 %copy.12.idx_ref = s32[128,6]{1,0:T(8,128)} copy(s32[128,6]{0,1:T(8,128)} %param.10) | data formatting | bytes 6144 | tf_op args[1]
  2.1 1.4 %copy.13.w_ref = f32[128,6]{1,0:T(8,128)} copy(f32[128,6]{0,1:T(8,128)} %param.11) | data formatting | bytes 6144 | tf_op args[2]
  3.5 0.0 copy-start
  3.5 2.7 %copy.14.gw_h = bf16[1,1024,704]{2,1,0:T(8,128)(2,1)} copy(bf16[1,1024,704]{1,2,0:T(8,128)(2,1)} %param.13) | data formatting | bytes 2883584 | tf_op args[4]
  6.2 0.0 copy-done
  6.2 1.6 %copy.15.uw_h = bf16[1,1024,704]{2,1,0:T(8,128)(2,1)} copy(bf16[1,1024,704]{1,2,0:T(8,128)(2,1)S(1)} %copy-done) | data formatting | bytes 2883584 | tf_op args[5]
  7.7 88.8 %shard_map.112 = (bf16[128,1024]{1,0:T(8,128)(2,1)}, bf16[1,16,704]{2,1,0:T(8,128)(2,1)}, bf16[1,16,1024]{2,1,0:T(8,128)(2,1)}) custom-call(bf16[128,1024]{1,0:T(8,128)(2,1)} %tok_h.1, s32[128,6]{1,0:T(8,128)} %copy.12.idx_ref, f32[128,6]{1,0:T(8,128)} %copy.13.w_ref, bf16[128,1024]{1,0:T(8,128)(2,1)} %og_ref.1, bf16[1,1024,704]{2,1,0:T(8,128)(2,1)} %copy.14.gw_h, ...), custom_call_target="tpu_custom_call" | custom-call | tf_op jit(solution)/shard_map/pallas_call | solution.py:446
  96.5 1.7 %copy.19 = bf16[128,1024]{1,0:T(8,128)(2,1)} copy(bf16[128,1024]{1,0:T(8,128)(2,1)} %get-tuple-element.6) | data formatting | bytes 524288
  98.2 1.3 %copy.20 = bf16[1,16,704]{2,1,0:T(8,128)(2,1)} copy(bf16[1,16,704]{2,1,0:T(8,128)(2,1)} %get-tuple-element.7) | data formatting | bytes 45056
  99.5 1.4 %copy.21 = bf16[1,16,1024]{2,1,0:T(8,128)(2,1)} copy(bf16[1,16,1024]{2,1,0:T(8,128)(2,1)} %get-tuple-element.8) | data formatting | bytes 65536
Async XLA Ops:
  3.5 2.7 %copy-start = (bf16[1,1024,704]{1,2,0:T(8,128)(2,1)S(1)}, bf16[1,1024,704]{1,2,0:T(8,128)(2,1)}, u32[]{:S(2)}) copy-start(bf16[1,1024,704]{1,2,0:T(8,128)(2,1)} %param.14) | copy-start | bytes 4325380

commit v3 on v2

--- a/solution.py
+++ b/solution.py
@@ -140,8 +140,7 @@
     )
 
     def spread_gates(e):
-        column = jnp.sum(jnp.where(idx_ref[...] == e, w_ref[...], 0.0), axis=1, keepdims=True)
-        row = jnp.sum(jnp.where(eye, column, 0.0), axis=0, keepdims=True)
+        row = jnp.sum(jnp.where(idx_ref[...] == e, w_ref[...], 0.0), axis=0, keepdims=True)
         gexp[e] = jnp.broadcast_to(row, (rank, rows))
 
     each(0, n, spread_gates)
@@ -227,8 +226,6 @@
     def arrived_mate(buf, sems, p):
         to_mate(buf.at[p], buf.at[p], sems.at[p], sems.at[p], p).wait_recv()
 
-    each(1, n, lambda s: gate_copy(s).start())
-    each(1, n, lambda s: au_copy(s).start())
     load_tok.wait()
 
     def spread(z, go_up, go_down):
@@ -243,6 +240,8 @@
         each(1, side, lambda s: side_copy(z, s).start())
 
     spread(at_line, True, True)
+    each(1, n, lambda s: gate_copy(s).start())
+    each(1, n, lambda s: au_copy(s).start())
     au_all[me] = au_ref[0]
     gate_recv[me] = gexp[me, 0:8]
 
@@ -252,8 +251,8 @@
 
     def expert_block(src):
         x = tok_all[src]
-        g = dot(x, gw[...])
-        u = dot(x, uw[...])
+        g = dot_nt(x, gw[...])
+        u = dot_nt(x, uw[...])
         h = (g / (1.0 + jnp.exp(-g)) * u).astype(BF16)
         hid_all[src] = h
         low_t = dot_nt(ad_ref[0], h).astype(BF16)
@@ -345,30 +344,35 @@
                 line_send[z] = pair_sum(z).astype(BF16)
                 line_copy(z).start()
 
+    def grads():
+        each(1, n, lambda s: arrived(lg_recv, lg_r, source(s)))
+
+        def add_gin(src, total):
+            return total + dot(lg_recv[src], hid_all[src])
+
+        gin_all[rep] = lax.fori_loop(0, n, add_gin, jnp.zeros(gin_all.shape[1:], F32))
+
+        each(1, n, lambda s: arrived(rk_recv, rk_r, source(s)))
+        low_w = (rk_recv[...].astype(F32) * gexp[...]).astype(BF16).reshape(n * rank, rows)
+        gp = dot(low_w, og_ref[...])
+        gp_send[...] = gp.astype(BF16).reshape(n, rank, width)
+        each(1, nd, lambda s: gin_copy(s).start())
+        gp_recv[me] = gp_send[me]
+        each(1, n, lambda s: gp_copy(peer(s)).start())
+
     def step(k):
         relay(k)
         each(0, 2 * side, lambda j: work(k, j))
-        pl.when(k == 0)(low_grads)
+        pl.when(k == 2)(low_grads)
+        pl.when(k == line + 1)(grads)
         combine(k)
 
     each(0, line + 2, step)
 
-    each(1, n, lambda s: arrived(lg_recv, lg_r, source(s)))
-
-    def add_gin(src, total):
-        return total + dot(lg_recv[src], hid_all[src])
-
-    gin_all[rep] = lax.fori_loop(0, n, add_gin, jnp.zeros(gin_all.shape[1:], F32))
-
-    each(1, n, lambda s: arrived(rk_recv, rk_r, source(s)))
-    low_w = (rk_recv[...].astype(F32) * gexp[...]).astype(BF16).reshape(n * rank, rows)
-    gp = dot(low_w, og_ref[...])
-    gp_send[...] = gp.astype(BF16).reshape(n, rank, width)
-    each(1, nd, lambda s: gin_copy(s).start())
-    gp_recv[me] = gp_send[me]
-    each(1, n, lambda s: gp_copy(peer(s)).start())
-
     acc[...] = pair_sum(at_line)
+    each(1, n, lambda s: arrived(gp_recv, gp_r, source(s)))
+    gout_all[rep] = jnp.sum(gp_recv[...].astype(F32), axis=0)
+    each(1, nd, lambda s: gout_copy(s).start())
 
     def finish(t):
         z = lax.rem(at_line + t, line)
@@ -378,11 +382,8 @@
     each(1, line, finish)
     mixed_ref[...] = acc[...].astype(BF16)
 
-    each(1, n, lambda s: arrived(gp_recv, gp_r, source(s)))
-    gout_all[rep] = jnp.sum(gp_recv[...].astype(F32), axis=0)
     each(1, nd, lambda s: arrived_mate(gin_all, gin_r, mate(s)))
     gin_ref[0] = jnp.sum(gin_all[...], axis=0).astype(BF16)
-    each(1, nd, lambda s: gout_copy(s).start())
     each(1, nd, lambda s: arrived_mate(gout_all, gout_r, mate(s)))
     gout_ref[0] = jnp.sum(gout_all[...], axis=0).astype(BF16)
 
@@ -422,6 +423,12 @@
         gout_copy(s).wait_send()
 
     each(1, nd, drain_mates)
+
+
+def hand_over(a_ref, b_ref, c_ref, x_ref, y_ref, z_ref):
+    x_ref[...] = a_ref[...]
+    y_ref[...] = b_ref[...]
+    z_ref[...] = c_ref[...]
 
 
 def shards(
@@ -443,7 +450,7 @@
     vmem = pl.BlockSpec(memory_space=pltpu.VMEM)
     anywhere = pl.BlockSpec(memory_space=pl.ANY)
     dma = pltpu.SemaphoreType.DMA
-    return pl.pallas_call(
+    results = pl.pallas_call(
         functools.partial(kernel, n, nd),
         out_shape=(
             jax.ShapeDtypeStruct((rows, width), BF16),
@@ -454,8 +461,8 @@
         out_specs=(vmem, vmem, vmem),
         scratch_shapes=[
             pltpu.VMEM((n, rows, width), BF16),
-            pltpu.VMEM((width, hidden), BF16),
-            pltpu.VMEM((width, hidden), BF16),
+            pltpu.VMEM((hidden, width), BF16),
+            pltpu.VMEM((hidden, width), BF16),
             pltpu.VMEM((hidden, width), BF16),
             pltpu.VMEM((n, rows, hidden), BF16),
             pltpu.VMEM((n, rows, width), BF16),
@@ -486,15 +493,21 @@
         ),
     )(
         tokens,
-        chosen_expert_index,
-        router_gate_weight,
+        chosen_expert_index.T,
+        router_gate_weight.T,
         output_gradient,
-        gate_weight_matrix,
-        up_weight,
+        jnp.swapaxes(gate_weight_matrix, 1, 2),
+        jnp.swapaxes(up_weight, 1, 2),
         down_weight,
         adapter_down_maps,
         adapter_up_maps,
     )
+    return pl.pallas_call(
+        hand_over,
+        out_shape=tuple(jax.ShapeDtypeStruct(r.shape, r.dtype) for r in results),
+        in_specs=[vmem] * 3,
+        out_specs=(vmem,) * 3,
+    )(*results)
 
 
 def solution(mesh):

time: 101 us -> 87.1 us (0.86)
  local copies, waits for them, and re-layouts: 11.5 us -> 0 us
  Pallas kernels: 88.8 us -> 86.3 us
    unnamed x9 -> x0, local copies, waits for them, and re-layouts: 11.5 us -> none
    pallas_call x1, Pallas kernels: 88.8 us -> 84.6 us  [shards(): pl.pallas_call(functools.partial(kernel, n, nd), out_shape=(jax.ShapeDtyp...]
    pallas_call x0 -> x1, Pallas kernels: none -> 1.7 us  [shards(): pl.pallas_call(hand_over, out_shape=tuple((jax.ShapeDtypeStruct(r.shape,...]
where the time goes in v3:
time: 87.1 us; the launch traced here: 87 us
  Pallas kernels  86.3 us (99%)
    pallas_call x1, Pallas kernels, shards(): pl.pallas_call(functools.partial(kernel, n, nd), out_shape=(jax.ShapeDtyp...  84.6 us

profile of v3, /device:TPU:1, one launch (start us, length us, event | category | flops | bytes accessed | tf_op | source)
XLA Modules:
  0.0 87.0 jit_solution(8299578758096478409)
XLA Ops:
  0.6 84.6 %shard_map.112 = (bf16[128,1024]{1,0:T(8,128)(2,1)}, bf16[1,16,704]{2,1,0:T(8,128)(2,1)}, bf16[1,16,1024]{2,1,0:T(8,128)(2,1)}) custom-call(bf16[128,1024]{1,0:T(8,128)(2,1)} %tok_h.1, s32[6,128]{1,0:T(8,128)} %bitcast.6, f32[6,128]{1,0:T(8,128)} %bitcast.7, bf16[128,1024]{1,0:T(8,128)(2,1)} %og_ref.1, bf16[1,704,1024]{2,1,0:T(8,128)(2,1)} %bitcast.4, ...), custom_call_target="tpu_custom_call" | custom-call | tf_op jit(solution)/shard_map/pallas_call | solution.py:453
  85.3 1.7 %shard_map.113 = (bf16[128,1024]{1,0:T(8,128)(2,1)}, bf16[1,16,704]{2,1,0:T(8,128)(2,1)}, bf16[1,16,1024]{2,1,0:T(8,128)(2,1)}) custom-call(bf16[128,1024]{1,0:T(8,128)(2,1)} %get-tuple-element.6.a_ref, bf16[1,16,704]{2,1,0:T(8,128)(2,1)} %get-tuple-element.7.b_ref, bf16[1,16,1024]{2,1,0:T(8,128)(2,1)} %get-tuple-element.8.c_ref), custom_call_target="tpu_custom_call" | custom-call | tf_op jit(solution)/shard_map/pallas_call | solution.py:505

commit v4 on v3

--- a/solution.py
+++ b/solution.py
@@ -241,7 +241,6 @@
 
     spread(at_line, True, True)
     each(1, n, lambda s: gate_copy(s).start())
-    each(1, n, lambda s: au_copy(s).start())
     au_all[me] = au_ref[0]
     gate_recv[me] = gexp[me, 0:8]
 
@@ -362,8 +361,9 @@
 
     def step(k):
         relay(k)
+        pl.when(k == 2)(lambda: each(1, n, lambda s: au_copy(s).start()))
         each(0, 2 * side, lambda j: work(k, j))
-        pl.when(k == 2)(low_grads)
+        pl.when(k == line)(low_grads)
         pl.when(k == line + 1)(grads)
         combine(k)
 

time: 87.1 us -> 88.9 us (1.021)
  Pallas kernels: 86.3 us -> 88.1 us
    pallas_call x1, Pallas kernels: 84.6 us -> 86.4 us  [shards(): pl.pallas_call(functools.partial(kernel, n, nd), out_shape=(jax.ShapeDtyp...]
where the time goes in v4:
time: 88.9 us; the launch traced here: 88.7 us
  Pallas kernels  88.1 us (99%)
    pallas_call x1, Pallas kernels, shards(): pl.pallas_call(functools.partial(kernel, n, nd), out_shape=(jax.ShapeDtyp...  86.4 us

profile of v4, /device:TPU:1, one launch (start us, length us, event | category | flops | bytes accessed | tf_op | source)
XLA Modules:
  0.0 88.7 jit_solution(481814526325821856)
XLA Ops:
  0.6 86.4 %shard_map.112 = (bf16[128,1024]{1,0:T(8,128)(2,1)}, bf16[1,16,704]{2,1,0:T(8,128)(2,1)}, bf16[1,16,1024]{2,1,0:T(8,128)(2,1)}) custom-call(bf16[128,1024]{1,0:T(8,128)(2,1)} %tok_h.1, s32[6,128]{1,0:T(8,128)} %bitcast.6, f32[6,128]{1,0:T(8,128)} %bitcast.7, bf16[128,1024]{1,0:T(8,128)(2,1)} %og_ref.1, bf16[1,704,1024]{2,1,0:T(8,128)(2,1)} %bitcast.4, ...), custom_call_target="tpu_custom_call" | custom-call | tf_op jit(solution)/shard_map/pallas_call | solution.py:453
  87.0 1.7 %shard_map.113 = (bf16[128,1024]{1,0:T(8,128)(2,1)}, bf16[1,16,704]{2,1,0:T(8,128)(2,1)}, bf16[1,16,1024]{2,1,0:T(8,128)(2,1)}) custom-call(bf16[128,1024]{1,0:T(8,128)(2,1)} %get-tuple-element.6.a_ref, bf16[1,16,704]{2,1,0:T(8,128)(2,1)} %get-tuple-element.7.b_ref, bf16[1,16,1024]{2,1,0:T(8,128)(2,1)} %get-tuple-element.8.c_ref), custom_call_target="tpu_custom_call" | custom-call | tf_op jit(solution)/shard_map/pallas_call | solution.py:505
